TPU v7x, 256 devices: a whole 4x4x8 slice. The times are simulated.
256 devices in a mesh: freq: 4 (over x_hi, core), rcv: 64 (over y, z, x_lo).
Axes of the slice: x: 4 (x_hi: 2, x_lo: 2; x = x_hi * 2 + x_lo), y: 4, z: 8, core: 2. Of those that a mesh axis runs over, the one named last changes fastest.
Arguments:
- reflection: bfloat16 [8, 2, 2560, 2560], P('freq', None, 'rcv'), may hold values from -5 to 5, as said below
- starts: int32 [2560, 192], P('rcv'), may hold values from 8 to 56
- focusing: float32 [8, 2560, 2, 192], P('freq', 'rcv'), may hold values from -6 to 6
- residual: float32 [8, 2560, 2, 192], P('freq', 'rcv'), may hold values from -6 to 6
- direction: float32 [8, 2560, 2, 192], P('freq', 'rcv'), may hold values from -6 to 6
- gradient: float32 [8, 2560, 2, 192], P('freq', 'rcv'), may hold values from -30 to 30
Outputs:
- new_focusing: float32 [8, 2560, 2, 192], P('freq', 'rcv')
- new_residual: float32 [8, 2560, 2, 192], P('freq', 'rcv')
- new_direction: float32 [8, 2560, 2, 192], P('freq', 'rcv')
- green_field: float32 [8, 2560, 2, 192], P('freq', 'rcv')
- focal_correlation: float32 [8, 2, 192], P('freq')
Inputs may be any that keep to these rules, and one draw needn't show every extreme that they name: Each frequency's matrix is symmetric in source and receiver: reflection[f, c, s, r] = reflection[f, c, r, s].
All inputs are finite; a program needn't handle non-finite values.
Results may differ from a plain program's by a relative error of at most 0.0003.
The roundings to bfloat16 on the way count: a program that leaves them out, or rounds other values in their place, can miss the bound.
Values may be sent and summed in bfloat16 or wider, within the bound.
A program may use at most 64 MiB of HBM per device.

v0:
```python
import math
import jax
import jax.numpy as jnp
from jax import lax
from jax.sharding import Mesh
from jax.sharding import PartitionSpec as P

N = 2560
F = 8
TS = 64
FREQ = ("freq_0", "freq_1")
RCV = ("rcv_0", "rcv_1", "rcv_2")
FREQ_RCV = ("freq_0", "freq_1", "rcv_0", "rcv_1", "rcv_2")
band_start = 5
tiny = 1e-06
highest = lax.Precision.HIGHEST


def in_order(pieces, dim):
    lengths = list(pieces.shape[1:])
    lengths[dim] *= pieces.shape[0]
    return jnp.moveaxis(pieces, 0, dim).reshape(lengths)


def sent_to_all(value, axis):
    count = lax.axis_size(axis)
    return lax.all_to_all(
        jnp.broadcast_to(value[None], (count, *value.shape)), axis, 0, 0, tiled=True
    )


def gather_directly(value, axis, dim):
    return in_order(sent_to_all(value, axis), dim)


def one_axis_at_a_time(value, axes):
    for axis in axes:
        value = lax.psum(value, axis)
    return value


def all_blocks(value, axes, sequence):
    pieces = value
    for k in sequence:
        pieces = lax.all_gather(pieces, axes[k])
    done = sequence[::-1]
    back = [done.index(k) for k in range(len(axes))]
    pieces = pieces.transpose(*back, *range(len(axes), pieces.ndim))
    return pieces.reshape(-1, *value.shape)


def gathered_by_axis(value, axes, sequence, dim):
    return in_order(all_blocks(value, axes, sequence), dim)


def of_everyone(value, axis):
    everything = sent_to_all(value, axis)
    return jnp.sum(everything, axis=0)


def tables(count, offset):
    times = jnp.arange(TS, dtype=jnp.float32)[:, None]
    bins = (jnp.arange(count, dtype=jnp.int32) + offset + band_start).astype(jnp.float32)[None, :]
    phase = 2.0 * jnp.pi * times * bins / TS
    return (jnp.cos(phase), jnp.sin(phase))


def contract_time(table, values):
    return jnp.einsum("tf,frk->trk", table, values, precision=highest)


def contract_back(table, values):
    return jnp.einsum("tf,trk->frk", table, values, precision=highest)


def time_gate(field, forward_cos, forward_sin, back_cos, back_sin, limits, complement):
    real_part = field[:, :, 0]
    imag_part = field[:, :, 1]
    time_real = contract_time(forward_cos, real_part) - contract_time(forward_sin, imag_part)
    time_imag = contract_time(forward_sin, real_part) + contract_time(forward_cos, imag_part)
    clock = jnp.arange(TS, dtype=jnp.int32)[:, None, None]
    window = (clock < limits[None]).astype(jnp.float32)
    if complement:
        window = 1.0 - window
    kept_real = window * time_real
    kept_imag = window * time_imag
    out_real = (contract_back(back_cos, kept_real) + contract_back(back_sin, kept_imag)) / TS
    out_imag = (contract_back(back_cos, kept_imag) - contract_back(back_sin, kept_real)) / TS
    return jnp.stack([out_real, out_imag], axis=2)


def combine(total, conjugate):
    if conjugate:
        out_real = total[:, 0, :, 0] + total[:, 1, :, 1]
        out_imag = total[:, 0, :, 1] - total[:, 1, :, 0]
    else:
        out_real = total[:, 0, :, 0] - total[:, 1, :, 1]
        out_imag = total[:, 0, :, 1] + total[:, 1, :, 0]
    return jnp.stack([out_real, out_imag], axis=2)


def per_device(reflection, starts, focusing, residual, direction, gradient):
    local_freq = reflection.shape[0]
    position = lax.axis_index(FREQ)
    cos_table, sin_table = tables(F, 0)
    own_cos, own_sin = tables(local_freq, position * local_freq)

    def gate(field, complement):
        whole = gather_directly(field, FREQ, 0)
        return time_gate(whole, cos_table, sin_table, own_cos, own_sin, starts, complement)

    def accumulate(piece):
        return jnp.einsum("fpnm,fmqk->fpnqk", reflection, piece, preferred_element_type=jnp.float32)

    direction_low = direction.astype(jnp.bfloat16)
    focusing_low = focusing.astype(jnp.bfloat16)
    aimed_total = accumulate(lax.all_gather(direction_low, RCV, axis=1, tiled=True))
    direction_image = combine(aimed_total, False)
    image = gate(direction_image, False)
    gamma, curvature = (
        one_axis_at_a_time(jnp.sum(gradient * gradient), FREQ_RCV),
        one_axis_at_a_time(jnp.sum(image * image), FREQ_RCV),
    )
    alpha = gamma / (curvature + tiny)
    new_focusing = focusing + alpha * direction
    new_residual = residual - alpha * image
    gated = gate(new_residual, False).astype(jnp.bfloat16)
    total = accumulate(gathered_by_axis(gated, RCV, (2, 0, 1), 1))
    new_gradient = combine(total, True)
    new_gamma = one_axis_at_a_time(jnp.sum(new_gradient * new_gradient), FREQ_RCV)
    new_direction = new_gradient + new_gamma / (gamma + tiny) * direction
    focus_total = accumulate(lax.all_gather(focusing_low, RCV, axis=1, tiled=True))
    focusing_image = combine(focus_total, False)
    green_field = gate(focusing_image + alpha * direction_image, True)
    corr_real = jnp.sum(
        green_field[:, :, 0] * new_focusing[:, :, 0] + green_field[:, :, 1] * new_focusing[:, :, 1],
        axis=1,
    )
    corr_imag = jnp.sum(
        green_field[:, :, 1] * new_focusing[:, :, 0] - green_field[:, :, 0] * new_focusing[:, :, 1],
        axis=1,
    )
    partial_corr = jnp.stack([corr_real, corr_imag], axis=1)
    focal_correlation = of_everyone(partial_corr, RCV) / math.sqrt(N)
    return (new_focusing, new_residual, new_direction, green_field, focal_correlation)


def solution(mesh):
    finer = Mesh(
        mesh.devices.reshape(2, 2, 4, 8, 2), ("freq_0", "freq_1", "rcv_0", "rcv_1", "rcv_2")
    )
    in_specs = (
        P(FREQ, None, RCV, None),
        P(RCV, None),
        P(FREQ, RCV, None, None),
        P(FREQ, RCV, None, None),
        P(FREQ, RCV, None, None),
        P(FREQ, RCV, None, None),
    )
    out_specs = (
        P(FREQ, RCV, None, None),
        P(FREQ, RCV, None, None),
        P(FREQ, RCV, None, None),
        P(FREQ, RCV, None, None),
        P(FREQ, None, None),
    )
    return jax.shard_map(
        per_device, mesh=finer, in_specs=in_specs, out_specs=out_specs, check_vma=False
    )
```

profile of v0, /device:TPU:4, one launch (start us, length us, event | category | flops | bytes accessed | tf_op | source)
XLA Modules:
  0.0 782.8 jit_solution(11673476122548457123)
XLA Ops:
  7.2 1.6 copy.290
  8.9 1.6 copy.289
  10.5 307.9 %all-gather.6.cloned.1.call-done = bf16[2,2560,2,192]{3,1,2,0:T(8,128)(2,1)} async-done(((bf16[2,40,2,192]{3,1,2,0:T(8,128)(2,1)}), bf16[2,2560,2,192]{3,1,2,0:T(8,128)(2,1)}) %all-gather.6.cloned.1.call-update) | async-done | bytes 3932176 | tf_op jit(solution)/shard_map/all_gather | solution.py:117
  318.5 3.5 fusion
  323.2 4.8 all-to-all-start
  328.8 12.3 %all-to-all-done = f32[4,2,40,2,192]{4,1,2,3,0:T(2,128)S(1)} async-done(((f32[4,2,40,2,192]{4,1,2,3,0:T(2,128)}), f32[4,2,40,2,192]{4,1,2,3,0:T(2,128)S(1)}, u32[]{:S(2)}, u32[]{:S(2)}) %all-to-all-start) | async-done | bytes 491552 | tf_op jit(solution)/shard_map/all_to_all | solution.py:27
  341.8 2.4 fusion.7
  344.1 2.5 add_select_fusion.1
  346.7 1.4 fusion.115
  349.5 2.4 fusion.8
  351.8 2.5 subtract_select_fusion.1
  354.4 1.6 fusion.103
  358.0 7.1 all-reduce.4
  365.1 3.1 all-reduce.3
  368.1 8.3 %all-reduce.1 = (f32[]{:T(128)}, f32[]{:T(128)}) all-reduce(f32[]{:T(128)} %get-tuple-element.38, f32[]{:T(128)} %get-tuple-element.39), channel_id=1, replica_groups=mesh['freq_0'=2,'freq_1'=2,'rcv_0'=4,'rcv_1'=8,'rcv_2'=2] {'rcv_0'}, use_global_device_ids=true, to_apply=%region_3.0 | all-reduce | flops 2 | bytes 16 | tf_op jit(solution)/shard_map/psum | solution.py:38
  376.5 20.8 %all-reduce = (f32[]{:T(128)}, f32[]{:T(128)}) all-reduce(f32[]{:T(128)} %get-tuple-element.34, f32[]{:T(128)} %get-tuple-element.35), channel_id=1, replica_groups=mesh['freq_0'=2,'freq_1'=2,'rcv_0'=4,'rcv_1'=8,'rcv_2'=2] {'rcv_1'}, use_global_device_ids=true, to_apply=%region_4.0 | all-reduce | flops 2 | bytes 16 | tf_op jit(solution)/shard_map/psum | solution.py:38
  397.3 5.8 all-reduce.2
  405.4 18.5 %all_to_all.20 = f32[4,2,40,2,192]{4,1,2,3,0:T(2,128)S(1)} all-to-all(f32[4,2,40,2,192]{4,1,2,3,0:T(2,128)S(1)} %broadcast_in_dim.9), channel_id=1, replica_groups=mesh['freq_0'=2,'freq_1'=2,'rcv_0'=4,'rcv_1'=8,'rcv_2'=2] {'freq_0','fre..., dimensions={0} | all-to-all | bytes 983040 | tf_op jit(solution)/shard_map/all_to_all | solution.py:27
  424.6 2.4 fusion.10
  427.0 2.5 subtract_select_fusion
  429.5 1.4 fusion.99
  430.9 2.4 fusion.9
  433.3 2.5 add_select_fusion
  437.2 1.8 fusion.101
  440.4 6.1 all_gather.23
  446.6 15.6 %all-gather = bf16[8,2,40,2,192]{4,2,3,1,0:T(8,128)(2,1)} all-gather(bf16[2,2,40,2,192]{4,2,3,1,0:T(8,128)(2,1)S(1)} %all_gather.23), channel_id=2, replica_groups=mesh['freq_0'=2,'freq_1'=2,'rcv_0'=4,'rcv_1'=8,'rcv_2'=2] {'rcv_0'}, dimensions={0}, use_global_device_ids=true | all-gather | bytes 614400 | tf_op jit(solution)/shard_map/all_gather | solution.py:45
  462.2 162.9 %all-gather.8.cloned.1.call-done = bf16[2,2560,2,192]{3,1,2,0:T(8,128)(2,1)} async-done(((bf16[2,40,2,192]{3,1,2,0:T(8,128)(2,1)}), bf16[2,2560,2,192]{3,1,2,0:T(8,128)(2,1)}) %all-gather.8.cloned.1.call-update) | async-done | bytes 3932176 | tf_op jit(solution)/shard_map/all_gather | solution.py:132
  625.1 3.5 fusion.2
  629.8 4.8 all-to-all-start.2
  635.3 7.9 %all-to-all-done.2 = f32[4,2,40,2,192]{4,1,2,3,0:T(2,128)S(1)} async-done(((f32[4,2,40,2,192]{4,1,2,3,0:T(2,128)}), f32[4,2,40,2,192]{4,1,2,3,0:T(2,128)S(1)}, u32[]{:S(2)}, u32[]{:S(2)}) %all-to-all-start.2) | async-done | bytes 491552 | tf_op jit(solution)/shard_map/all_to_all | solution.py:27
  643.9 2.4 fusion.11
  646.3 3.9 fusion.12
  650.1 3.7 add_multiply_fusion
  653.8 34.5 %all-gather.10.cloned.1.call-done = bf16[32,2,2,40,2,192]{5,3,4,2,1,0:T(8,128)(2,1)} async-done(((bf16[4,2,2,40,2,192]{5,3,4,2,1,0:T(8,128)(2,1)}), bf16[32,2,2,40,2,192]{5,3,4,2,1,0:T(8,128)(2,1)}) %all-gather.10.cloned.1.call-update) | async-done | bytes 3932176 | tf_op jit(solution)/shard_map/all_gather | solution.py:45
  688.3 3.0 copy.180
  694.3 4.3 subtract_multiply_fusion
  698.6 7.1 psum.115
  705.7 3.8 fusion.109
  709.4 3.3 psum.116
  712.7 3.7 fusion.95
  716.4 11.1 %psum.117 = f32[]{:T(128)} all-reduce(f32[]{:T(128)} %psum.116), channel_id=1, replica_groups=mesh['freq_0'=2,'freq_1'=2,'rcv_0'=4,'rcv_1'=8,'rcv_2'=2] {'rcv_0'}, use_global_device_ids=true, to_apply=%region_15.0 | all-reduce | flops 1 | bytes 8 | tf_op jit(solution)/shard_map/psum | solution.py:38
  727.5 2.0 fusion.97
  729.5 16.1 %psum.118 = f32[]{:T(128)} all-reduce(f32[]{:T(128)} %psum.117), channel_id=1, replica_groups=mesh['freq_0'=2,'freq_1'=2,'rcv_0'=4,'rcv_1'=8,'rcv_2'=2] {'rcv_1'}, use_global_device_ids=true, to_apply=%region_16.0 | all-reduce | flops 1 | bytes 8 | tf_op jit(solution)/shard_map/psum | solution.py:38
  745.7 2.0 fusion.107
  747.7 5.5 psum.119
  756.9 7.5 all-to-all-start.3
  764.3 1.7 copy.198
  768.4 6.9 all-to-all-done.3
  (74 shorter events, 21.5 us)
Async XLA Ops:
  7.2 311.3 %copy-start = (bf16[2,2,40,2560]{3,2,1,0:T(8,128)(2,1)S(1)}, bf16[2,2,40,2560]{3,2,1,0:T(8,128)(2,1)}, u32[]{:S(2)}) copy-start(bf16[2,2,40,2560]{3,2,1,0:T(8,128)(2,1)} %param.6) | copy-start | bytes 2457604
  7.2 311.3 %all-gather.6.cloned.1.call-start = ((), (), s32[]{:S(2)}) async-start(), calls=%async_computation.4 | async-start | bytes 5324800 | tf_op jit(solution)/shard_map/all_gather | solution.py:117
  8.9 616.2 %all-gather.8.cloned.1.call-start = ((), (), s32[]{:S(2)}) async-start(), calls=%async_computation.5 | async-start | bytes 5324800 | tf_op jit(solution)/shard_map/all_gather | solution.py:132
  322.0 6.0 copy-start.8
  323.2 17.9 %all-to-all-start = ((f32[4,2,40,2,192]{4,1,2,3,0:T(2,128)}), f32[4,2,40,2,192]{4,1,2,3,0:T(2,128)S(1)}, u32[]{:S(2)}, u32[]{:S(2)}) async-start(f32[4,2,40,2,192]{4,1,2,3,0:T(2,128)} %broadcast_in_dim.8), calls=%async_computation | async-start | bytes 1310720 | tf_op jit(solution)/shard_map/all_to_all | solution.py:27
  328.0 360.4 %all-gather.10.cloned.1.call-start = ((), (), s32[]{:S(2)}) async-start(), calls=%async_computation.6 | async-start | bytes 5898240 | tf_op jit(solution)/shard_map/all_gather | solution.py:45
  328.8 15.4 %copy-start.4 = (s32[40,192]{1,0:T(8,128)S(1)}, s32[40,192]{1,0:T(8,128)}, u32[]{:S(2)}) copy-start(s32[40,192]{1,0:T(8,128)} %param.7) | copy-start | bytes 92164
  354.4 50.0 %copy-start.9 = (f32[2,40,2,192]{3,2,1,0:T(2,128)S(1)}, f32[2,40,2,192]{3,2,1,0:T(2,128)}, u32[]{:S(2)}) copy-start(f32[2,40,2,192]{3,2,1,0:T(2,128)} %param.9) | copy-start | bytes 368644
  404.4 0.7 copy-start.5
  629.8 13.4 %all-to-all-start.2 = ((f32[4,2,40,2,192]{4,1,2,3,0:T(2,128)}), f32[4,2,40,2,192]{4,1,2,3,0:T(2,128)S(1)}, u32[]{:S(2)}, u32[]{:S(2)}) async-start(f32[4,2,40,2,192]{4,1,2,3,0:T(2,128)} %broadcast_in_dim.10), calls=%async_computation.2 | async-start | bytes 1310720 | tf_op jit(solution)/shard_map/all_to_all | solution.py:27
  643.9 2.4 copy-start.2
  691.4 3.0 copy-start.1
  691.4 3.0 copy-start.3
  692.4 0.6 copy-start.6
  693.1 0.6 copy-start.7
  756.9 18.5 %all-to-all-start.3 = ((f32[64,2,2,192]{3,2,1,0:T(2,128)}), f32[64,2,2,192]{3,2,1,0:T(2,128)S(1)}, u32[]{:S(2)}, u32[]{:S(2)}) async-start(f32[64,2,2,192]{3,2,1,0:T(2,128)} %broadcast_in_dim.11), calls=%async_computation.3 | async-start | bytes 524288 | tf_op jit(solution)/shard_map/all_to_all | solution.py:27
Sparse Core Ops, SparseCore 0:
  10.4 308.0 all-gather.5
  320.8 304.2 all-gather.7
  626.9 61.3 all-gather.9
where the time goes:
time: 793 us; the launch traced here: 783 us
  waiting for transfers between devices  533 us (67%)
  blocking collectives  128 us (16%)
  matrix products  65.1 us (8%)
  local copies, waits for them, and re-layouts  17.5 us (2%)
  starting transfers between devices  17.1 us (2%)
  between operations  16.9 us (2%)
    all_gather x1, waiting for transfers between devices, per_device(): lax.all_gather(direction_low, RCV, axis=1, tiled=True)  308 us
    all_gather x1, waiting for transfers between devices, per_device(): lax.all_gather(focusing_low, RCV, axis=1, tiled=True)  163 us
    psum x10, blocking collectives, one_axis_at_a_time(): value = lax.psum(value, axis)  88.1 us
    all_gather x1, waiting for transfers between devices, all_blocks(): pieces = lax.all_gather(pieces, axes[k])  34.5 us
    dot_general x12, matrix products, contract_time(): return jnp.einsum('tf,frk->trk', table, values, precision=highest)  33.8 us
    all_to_all x3, waiting for transfers between devices, sent_to_all(): lax.all_to_all(jnp.broadcast_to(value[None], (count, *value.shape)), axis...  27.2 us
    dot_general x12, matrix products, contract_back(): return jnp.einsum('tf,trk->frk', table, values, precision=highest)  23.2 us
    all_gather x2, blocking collectives, all_blocks(): pieces = lax.all_gather(pieces, axes[k])  21.7 us
  transfers between devices with their start and end apart: 6, of which 6 were waited for; matrix products, arithmetic and copies ran while one was open for 8% of the time, Pallas kernels for 0%

commit v1 on v0

--- a/solution.py
+++ b/solution.py
@@ -114,7 +114,7 @@
 
     direction_low = direction.astype(jnp.bfloat16)
     focusing_low = focusing.astype(jnp.bfloat16)
-    aimed_total = accumulate(lax.all_gather(direction_low, RCV, axis=1, tiled=True))
+    aimed_total = accumulate(jnp.concatenate(lax.all_gather(direction_low, RCV), axis=1))
     direction_image = combine(aimed_total, False)
     image = gate(direction_image, False)
     gamma, curvature = (

time: 793 us -> 792 us (level)
  no operation moved by 1% of the time
where the time goes in v1:
time: 792 us; the launch traced here: 781 us
  waiting for transfers between devices  531 us (67%)
  blocking collectives  128 us (16%)
  matrix products  62.6 us (8%)
  local copies, waits for them, and re-layouts  20.3 us (3%)
  starting transfers between devices  17.2 us (2%)
  between operations  16.9 us (2%)
    all_gather x1, waiting for transfers between devices, per_device(): lax.all_gather(direction_low, RCV)  308 us
    all_gather x1, waiting for transfers between devices, per_device(): lax.all_gather(focusing_low, RCV, axis=1, tiled=True)  162 us
    psum x10, blocking collectives, one_axis_at_a_time(): value = lax.psum(value, axis)  87.7 us
    all_gather x1, waiting for transfers between devices, all_blocks(): pieces = lax.all_gather(pieces, axes[k])  33.8 us
    dot_general x12, matrix products, contract_time(): return jnp.einsum('tf,frk->trk', table, values, precision=highest)  33.8 us
    all_to_all x3, waiting for transfers between devices, sent_to_all(): lax.all_to_all(jnp.broadcast_to(value[None], (count, *value.shape)), axis...  27.4 us
    dot_general x12, matrix products, contract_back(): return jnp.einsum('tf,trk->frk', table, values, precision=highest)  23.2 us
    all_gather x2, blocking collectives, all_blocks(): pieces = lax.all_gather(pieces, axes[k])  22.1 us
  transfers between devices with their start and end apart: 6, of which 6 were waited for; matrix products, arithmetic and copies ran while one was open for 8% of the time, Pallas kernels for 0%

profile of v1, /device:TPU:4, one launch (start us, length us, event | category | flops | bytes accessed | tf_op | source)
XLA Modules:
  0.0 781.4 jit_solution(5329306321623116794)
XLA Ops:
  7.2 1.6 copy.299
  8.9 1.6 copy.298
  10.5 308.0 %all-gather.9.cloned.1.call-done = bf16[128,40,2,192]{3,1,2,0:T(8,128)(2,1)} async-done(((bf16[2,40,2,192]{3,1,2,0:T(8,128)(2,1)}), bf16[128,40,2,192]{3,1,2,0:T(8,128)(2,1)}) %all-gather.9.cloned.1.call-update) | async-done | bytes 3932176 | tf_op jit(solution)/shard_map/all_gather | solution.py:117
  318.5 2.8 copy.167
  323.6 4.8 all-to-all-start
  329.2 12.5 %all-to-all-done = f32[4,2,40,2,192]{4,1,2,3,0:T(2,128)S(1)} async-done(((f32[4,2,40,2,192]{4,1,2,3,0:T(2,128)}), f32[4,2,40,2,192]{4,1,2,3,0:T(2,128)S(1)}, u32[]{:S(2)}, u32[]{:S(2)}) %all-to-all-start) | async-done | bytes 491552 | tf_op jit(solution)/shard_map/all_to_all | solution.py:27
  342.4 2.4 fusion.6
  344.7 2.5 add_select_fusion.1
  347.3 1.4 fusion.114
  350.0 2.4 fusion.7
  352.4 2.5 subtract_select_fusion.1
  355.0 1.6 fusion.102
  358.6 7.1 all-reduce.4
  365.6 3.1 all-reduce.3
  368.7 8.3 %all-reduce.1 = (f32[]{:T(128)}, f32[]{:T(128)}) all-reduce(f32[]{:T(128)} %get-tuple-element.38, f32[]{:T(128)} %get-tuple-element.39), channel_id=1, replica_groups=mesh['freq_0'=2,'freq_1'=2,'rcv_0'=4,'rcv_1'=8,'rcv_2'=2] {'rcv_0'}, use_global_device_ids=true, to_apply=%region_3.0 | all-reduce | flops 2 | bytes 16 | tf_op jit(solution)/shard_map/psum | solution.py:38
  377.1 20.4 %all-reduce = (f32[]{:T(128)}, f32[]{:T(128)}) all-reduce(f32[]{:T(128)} %get-tuple-element.34, f32[]{:T(128)} %get-tuple-element.35), channel_id=1, replica_groups=mesh['freq_0'=2,'freq_1'=2,'rcv_0'=4,'rcv_1'=8,'rcv_2'=2] {'rcv_1'}, use_global_device_ids=true, to_apply=%region_4.0 | all-reduce | flops 2 | bytes 16 | tf_op jit(solution)/shard_map/psum | solution.py:38
  397.5 5.8 all-reduce.2
  405.5 18.3 %all_to_all.20 = f32[4,2,40,2,192]{4,1,2,3,0:T(2,128)S(1)} all-to-all(f32[4,2,40,2,192]{4,1,2,3,0:T(2,128)S(1)} %broadcast_in_dim.9), channel_id=1, replica_groups=mesh['freq_0'=2,'freq_1'=2,'rcv_0'=4,'rcv_1'=8,'rcv_2'=2] {'freq_0','fre..., dimensions={0} | all-to-all | bytes 983040 | tf_op jit(solution)/shard_map/all_to_all | solution.py:27
  424.5 2.4 fusion.9
  426.9 2.5 subtract_select_fusion
  429.4 1.4 fusion.98
  430.8 2.4 fusion.8
  433.2 2.5 add_select_fusion
  437.1 1.8 fusion.100
  440.4 6.6 all_gather.27
  446.9 15.5 %all-gather.1 = bf16[8,2,40,2,192]{4,2,3,1,0:T(8,128)(2,1)} all-gather(bf16[2,2,40,2,192]{4,2,3,1,0:T(8,128)(2,1)S(1)} %all_gather.27), channel_id=3, replica_groups=mesh['freq_0'=2,'freq_1'=2,'rcv_0'=4,'rcv_1'=8,'rcv_2'=2] {'rcv_0'}, dimensions={0}, use_global_device_ids=true | all-gather | bytes 614400 | tf_op jit(solution)/shard_map/all_gather | solution.py:45
  462.5 161.8 %all-gather.7.cloned.1.call-done = bf16[2,2560,2,192]{3,1,2,0:T(8,128)(2,1)} async-done(((bf16[2,40,2,192]{3,1,2,0:T(8,128)(2,1)}), bf16[2,2560,2,192]{3,1,2,0:T(8,128)(2,1)}) %all-gather.7.cloned.1.call-update) | async-done | bytes 3932176 | tf_op jit(solution)/shard_map/all_gather | solution.py:132
  624.2 3.5 fusion
  629.0 4.8 all-to-all-start.2
  634.4 7.9 %all-to-all-done.2 = f32[4,2,40,2,192]{4,1,2,3,0:T(2,128)S(1)} async-done(((f32[4,2,40,2,192]{4,1,2,3,0:T(2,128)}), f32[4,2,40,2,192]{4,1,2,3,0:T(2,128)S(1)}, u32[]{:S(2)}, u32[]{:S(2)}) %all-to-all-start.2) | async-done | bytes 491552 | tf_op jit(solution)/shard_map/all_to_all | solution.py:27
  643.0 2.4 fusion.10
  645.4 3.9 fusion.11
  649.3 3.7 add_multiply_fusion
  653.0 33.8 %all-gather.11.cloned.1.call-done = bf16[32,2,2,40,2,192]{5,3,4,2,1,0:T(8,128)(2,1)} async-done(((bf16[4,2,2,40,2,192]{5,3,4,2,1,0:T(8,128)(2,1)}), bf16[32,2,2,40,2,192]{5,3,4,2,1,0:T(8,128)(2,1)}) %all-gather.11.cloned.1.call-update) | async-done | bytes 3932176 | tf_op jit(solution)/shard_map/all_gather | solution.py:45
  686.8 3.0 copy.187
  692.8 4.3 subtract_multiply_fusion
  697.1 7.1 psum.115
  704.2 3.8 fusion.108
  707.9 3.3 psum.116
  711.2 3.7 fusion.94
  714.9 11.1 %psum.117 = f32[]{:T(128)} all-reduce(f32[]{:T(128)} %psum.116), channel_id=1, replica_groups=mesh['freq_0'=2,'freq_1'=2,'rcv_0'=4,'rcv_1'=8,'rcv_2'=2] {'rcv_0'}, use_global_device_ids=true, to_apply=%region_15.0 | all-reduce | flops 1 | bytes 8 | tf_op jit(solution)/shard_map/psum | solution.py:38
  726.0 2.0 fusion.96
  728.0 16.1 %psum.118 = f32[]{:T(128)} all-reduce(f32[]{:T(128)} %psum.117), channel_id=1, replica_groups=mesh['freq_0'=2,'freq_1'=2,'rcv_0'=4,'rcv_1'=8,'rcv_2'=2] {'rcv_1'}, use_global_device_ids=true, to_apply=%region_16.0 | all-reduce | flops 1 | bytes 8 | tf_op jit(solution)/shard_map/psum | solution.py:38
  744.1 2.0 fusion.106
  746.2 5.5 psum.119
  755.4 7.5 all-to-all-start.3
  762.9 1.7 copy.205
  767.0 6.9 all-to-all-done.3
  (75 shorter events, 22.5 us)
Async XLA Ops:
  7.2 314.2 %copy-start = (bf16[2,2,40,2560]{3,2,1,0:T(8,128)(2,1)S(1)}, bf16[2,2,40,2560]{3,2,1,0:T(8,128)(2,1)}, u32[]{:S(2)}) copy-start(bf16[2,2,40,2560]{3,2,1,0:T(8,128)(2,1)} %param.6) | copy-start | bytes 2457604
  7.2 311.3 %all-gather.9.cloned.1.call-start = ((), (), s32[]{:S(2)}) async-start(), calls=%async_computation.5 | async-start | bytes 5324800 | tf_op jit(solution)/shard_map/all_gather | solution.py:117
  8.9 615.4 %all-gather.7.cloned.1.call-start = ((), (), s32[]{:S(2)}) async-start(), calls=%async_computation.4 | async-start | bytes 5324800 | tf_op jit(solution)/shard_map/all_gather | solution.py:132
  322.4 6.0 copy-start.8
  323.6 18.1 %all-to-all-start = ((f32[4,2,40,2,192]{4,1,2,3,0:T(2,128)}), f32[4,2,40,2,192]{4,1,2,3,0:T(2,128)S(1)}, u32[]{:S(2)}, u32[]{:S(2)}) async-start(f32[4,2,40,2,192]{4,1,2,3,0:T(2,128)} %broadcast_in_dim.8), calls=%async_computation | async-start | bytes 1310720 | tf_op jit(solution)/shard_map/all_to_all | solution.py:27
  328.4 358.4 %all-gather.11.cloned.1.call-start = ((), (), s32[]{:S(2)}) async-start(), calls=%async_computation.6 | async-start | bytes 5898240 | tf_op jit(solution)/shard_map/all_gather | solution.py:45
  329.2 15.6 %copy-start.4 = (s32[40,192]{1,0:T(8,128)S(1)}, s32[40,192]{1,0:T(8,128)}, u32[]{:S(2)}) copy-start(s32[40,192]{1,0:T(8,128)} %param.7) | copy-start | bytes 92164
  354.9 49.6 %copy-start.9 = (f32[2,40,2,192]{3,2,1,0:T(2,128)S(1)}, f32[2,40,2,192]{3,2,1,0:T(2,128)}, u32[]{:S(2)}) copy-start(f32[2,40,2,192]{3,2,1,0:T(2,128)} %param.9) | copy-start | bytes 368644
  404.6 0.7 copy-start.5
  629.0 13.4 %all-to-all-start.2 = ((f32[4,2,40,2,192]{4,1,2,3,0:T(2,128)}), f32[4,2,40,2,192]{4,1,2,3,0:T(2,128)S(1)}, u32[]{:S(2)}, u32[]{:S(2)}) async-start(f32[4,2,40,2,192]{4,1,2,3,0:T(2,128)} %broadcast_in_dim.10), calls=%async_computation.2 | async-start | bytes 1310720 | tf_op jit(solution)/shard_map/all_to_all | solution.py:27
  643.0 2.4 copy-start.2
  689.8 3.0 copy-start.1
  689.8 3.0 copy-start.3
  690.9 0.6 copy-start.6
  691.5 0.6 copy-start.7
  755.4 18.6 %all-to-all-start.3 = ((f32[64,2,2,192]{3,2,1,0:T(2,128)}), f32[64,2,2,192]{3,2,1,0:T(2,128)S(1)}, u32[]{:S(2)}, u32[]{:S(2)}) async-start(f32[64,2,2,192]{3,2,1,0:T(2,128)} %broadcast_in_dim.11), calls=%async_computation.3 | async-start | bytes 524288 | tf_op jit(solution)/shard_map/all_to_all | solution.py:27
Sparse Core Ops, SparseCore 0:
  10.3 308.1 all-gather.8
  320.9 303.3 all-gather.6
  626.0 60.7 all-gather.10
